TPU v7x, 32 devices: a whole 2x2x4 slice. The times are simulated.
32 devices in a mesh: seq: 8 (over z, y), head: 4 (over x, core).
Axes of the slice: x: 2, y: 2, z: 4, core: 2. Of those that a mesh axis runs over, the one named last changes fastest.
Arguments:
- query: bfloat16 [128, 32, 128], P(None, 'head'), may hold values from -8 to 8
- key_cache: bfloat16 [16384, 16, 128], P('seq', 'head'), may hold values from -6 to 6
- value_cache: bfloat16 [16384, 16, 128], P('seq', 'head'), may hold values from -6 to 6
- lengths: int32 [8], P('seq'), may hold values from 1 to 2048, 12288 in all
- out_weight: bfloat16 [4608, 4096], P('seq', 'head'), may hold values from -10 to 10
- norm_gain: float32 [4608], P('seq'), may hold values from 0.1 to 1.9
Outputs:
- normed: bfloat16 [128, 4608], P(None, 'seq')
Inputs may be any that keep to these rules, and one draw needn't show every extreme that they name: `lengths`: every block has at least one valid position, and some block is valid throughout.
All inputs are finite; a program needn't handle non-finite values.
Results may differ from a plain program's by a relative error of at most 0.0083.
Values may be sent and summed in bfloat16 or wider, within the bound.
A program may use at most 128 MiB of HBM per device.

v0:
```python
import jax
import jax.numpy as jnp
from jax import lax
from jax.sharding import PartitionSpec as P

D = 4608
QPRE = 144


def merged(value, axis, join):
    pieces = jax.tree.map(lambda part: lax.all_gather(part, axis), value)
    head = jax.tree.map(lambda part: part[0], pieces)
    tail = jax.tree.map(lambda part: part[1:], pieces)
    so_far, _ = lax.scan(lambda so_far, share: (join(so_far, share), None), head, tail)
    return so_far


def combine_partials(former, latter):
    max_former, sum_former, acc_former = former
    max_latter, sum_latter, acc_latter = latter
    new_max = jnp.maximum(max_former, max_latter)
    factor_former = jnp.exp(max_former - new_max)
    factor_latter = jnp.exp(max_latter - new_max)
    new_sum = factor_former * sum_former + factor_latter * sum_latter
    new_acc = factor_former[..., None] * acc_former + factor_latter[..., None] * acc_latter
    return (new_max, new_sum, new_acc)


def body(query, key_cache, value_cache, lengths, out_weight, norm_gain):
    tok_count, heads_local, head_dim = query.shape
    key_count, kv_local, unused_dim = key_cache.shape
    group_size = heads_local // kv_local
    score_scale = float(QPRE) ** (-0.5)
    grouped = query.reshape(tok_count, kv_local, group_size, head_dim)
    scores = (
        jnp.einsum("tkgd,ckd->kgtc", grouped, key_cache, preferred_element_type=jnp.float32)
        * score_scale
    )
    inside = lax.iota(jnp.int32, key_count) < lengths[0]
    scores = jnp.where(inside, scores, jnp.float32(-1e30))
    block_max = jnp.max(scores, axis=-1)
    weights = jnp.where(inside, jnp.exp(scores - block_max[..., None]), jnp.float32(0.0))
    block_sum = jnp.sum(weights, axis=-1)
    weights_low = weights.astype(jnp.bfloat16)
    weighted = jnp.einsum(
        "kgtc,ckd->tkgd", weights_low, value_cache, preferred_element_type=jnp.float32
    )
    weighted = weighted.reshape(tok_count, heads_local, head_dim)
    block_max = jnp.transpose(block_max, (2, 0, 1)).reshape(tok_count, heads_local)
    block_sum = jnp.transpose(block_sum, (2, 0, 1)).reshape(tok_count, heads_local)
    peak_all, total_all, combined = merged(
        (block_max, block_sum, weighted), "seq", combine_partials
    )
    attention = (
        (combined / total_all[..., None])
        .reshape(tok_count, heads_local * head_dim)
        .astype(jnp.bfloat16)
    )
    projected_part = lax.dot_general(
        attention, out_weight, (((1,), (1,)), ((), ())), preferred_element_type=jnp.float32
    )
    projected = lax.psum(projected_part, "head")
    square_part = jnp.sum(projected * projected, axis=-1)
    square_total = lax.psum(square_part, "seq")
    mean_square = square_total / D
    normed = projected * lax.rsqrt(mean_square + 1e-06)[:, None] * norm_gain[None, :]
    return normed.astype(jnp.bfloat16)


def solution(mesh):
    placed = (
        P(None, "head", None),
        P("seq", "head", None),
        P("seq", "head", None),
        P("seq"),
        P("seq", "head"),
        P("seq"),
    )
    return jax.shard_map(
        body, mesh=mesh, in_specs=placed, out_specs=P(None, "seq"), check_vma=False
    )
```

profile of v0, /device:TPU:0, one launch (start us, length us, event | category | flops | bytes accessed | tf_op | source)
XLA Modules:
  0.0 174.1 jit_solution(1487944032741304655)
XLA Ops:
  7.4 3.9 %bitcast_reduce_fusion = (f32[4,2,128]{2,1,0:T(2,128)S(1)}, f32[4,2048,128,2]{2,1,3,0:T(8,128)S(1)}) fusion(pred[2048]{0:T(1024)(128)(4,1)S(1)} %iota_compare_fusion, bf16[128,4,2,128]{3,2,1,0:T(2,128)(2,1)} %bitcast.62, bf16[2048,4,128,1]{2,1,0,3:T(4,128)(2,1)} %bitcast.61), kind=kOutput, calls=%fused_computation.9 | convolution fusion | flops 543161344 | bytes 10754048 | tf_op jit(solution)/shard_map/tkgd,ckd->kgtc/dot_general | solution.py:36
  11.2 3.4 %fusion.7 = f32[4,2,128,128]{3,2,1,0:T(8,128)S(1)} fusion(f32[4,2048,128,2]{2,1,3,0:T(8,128)S(1)} %get-tuple-element.64, f32[4,2,128]{2,1,0:T(2,128)S(1)} %get-tuple-element.63, pred[2048]{0:T(1024)(128)(4,1)S(1)} %iota_compare_fusion, bf16[2048,4,128,1]{2,1,0,3:T(4,128)(2,1)S(1)} %bitcast.56), kind=kOutput, calls=%fused_computation.15 | convolution fusion | flops 547356672 | bytes 11016192 | tf_op jit(solution)/shard_map/kgtc,ckd->tkgd/dot_general | solution.py:45
  14.7 1.1 copy.21
  15.9 4.6 %fusion.6 = f32[4,2,128]{2,1,0:T(2,128)S(1)} fusion(f32[4,2048,128,2]{2,1,3,0:T(8,128)} %copy-done.1, f32[4,2,128]{2,1,0:T(2,128)S(1)} %get-tuple-element.63, pred[2048]{0:T(1024)(128)(4,1)S(1)} %iota_compare_fusion), kind=kLoop, calls=%fused_computation.14 | loop fusion | flops 10484736 | bytes 8398848 | tf_op jit(solution)/shard_map/reduce_sum | solution.py:43
  20.5 33.0 %all_gather.10 = f32[8,128,8]{1,2,0:T(8,128)S(1)} all-gather(f32[1,128,8]{1,2,0:T(8,128)S(1)} %bitcast.60), channel_id=1, replica_groups=mesh['seq'=8,'head'=4] {'seq'}, dimensions={0}, use_global_device_ids=true | all-gather | bytes 36864 | tf_op jit(solution)/shard_map/all_gather | solution.py:11
  53.5 31.8 %all_gather.9 = f32[8,128,8]{1,2,0:T(8,128)S(1)} all-gather(f32[1,128,8]{1,2,0:T(8,128)S(1)} %bitcast.59), channel_id=1, replica_groups=mesh['seq'=8,'head'=4] {'seq'}, dimensions={0}, use_global_device_ids=true | all-gather | bytes 36864 | tf_op jit(solution)/shard_map/all_gather | solution.py:11
  85.3 6.9 %all-gather.2.cloned.1.call-done = f32[8,128,8,128]{3,2,1,0:T(8,128)} async-done(((f32[1,128,8,128]{3,2,1,0:T(8,128)}), f32[8,128,8,128]{3,2,1,0:T(8,128)}) %all-gather.2.cloned.1.call-update) | async-done | bytes 4194320 | tf_op jit(solution)/shard_map/all_gather | solution.py:11
  92.2 1.1 slice_bitcast_fusion
  93.3 4.1 %slice.29 = f32[7,128,8,128]{3,2,1,0:T(8,128)} slice(f32[8,128,8,128]{3,2,1,0:T(8,128)} %all-gather.2.cloned.1.call-done), slice={[1:8], [0:128], [0:8], [0:128]} | slice | bytes 7340032 | tf_op jit(solution)/shard_map/slice | solution.py:13
  97.4 11.7 %while.14 = (s32[]{:T(128)}, f32[128,8]{0,1:T(8,128)S(1)}, f32[128,8]{0,1:T(8,128)S(1)}, f32[128,8,128]{2,1,0:T(8,128)S(1)}, f32[7,128,8]{1,2,0:T(8,128)S(1)}, /...) while((s32[]{:T(128)}, f32[128,8]{0,1:T(8,128)S(1)}, f32[128,8]{0,1:T(8,128)S(1)}, ...), condition=%wide.region_3.4_spmd, body=%wide.region_2.3_spmd.sunk | while | flops 399362 | bytes 1630309 | solution.py:14
  97.4 0.1 copy.47
  97.6 1.4 fusion.26
  99.3 1.4 fusion.26
  100.9 1.4 fusion.26
  102.6 1.4 fusion.26
  104.3 1.4 fusion.26
  106.0 1.4 fusion.26
  107.7 1.4 fusion.26
  109.2 0.2 divide_convert_fusion
  109.4 2.5 %fusion.14 = f32[128,576]{0,1:T(8,128)} fusion(bf16[576,1024]{1,0:T(8,128)(2,1)} %param.12, bf16[16,8,8,128]{3,2,1,0:T(8,128)(2,1)S(1)} %bitcast.57), kind=kOutput, calls=%fused_computation.25 | convolution fusion | flops 150994944 | bytes 1736704 | tf_op jit(solution)/shard_map/dot_general | solution.py:59
  111.9 31.2 %all-reduce.2.cloned.1.call-done = f32[128,576]{0,1:T(8,128)} async-done(((f32[128,576]{0,1:T(8,128)}), f32[128,576]{0,1:T(8,128)}) %all-reduce.2.cloned.1.call-update) | async-done | bytes 294928 | tf_op jit(solution)/shard_map/psum | solution.py:62
  143.1 1.1 multiply_reduce_fusion
  144.2 21.4 %psum.15 = f32[128]{0:T(128)S(1)} all-reduce(f32[128]{0:T(128)S(1)} %multiply_reduce_fusion), channel_id=1, replica_groups=mesh['seq'=8,'head'=4] {'seq'}, use_global_device_ids=true, to_apply=%region_6.7 | all-reduce | flops 128 | bytes 1024 | tf_op jit(solution)/shard_map/psum | solution.py:64
  165.5 1.8 %multiply_convert_fusion = bf16[128,576]{0,1:T(8,128)(2,1)} fusion(f32[128,576]{0,1:T(8,128)} %all-reduce.2.cloned.1.call-done, f32[576]{0:T(1024)S(1)} %copy-done.2, f32[128]{0:T(128)S(1)} %add_rsqrt_fusion), kind=kLoop, calls=%fused_computation.23 | loop fusion | flops 221184 | bytes 445184 | tf_op jit(solution)/shard_map/convert_element_type | solution.py:67
  (37 shorter events, 1.7 us)
Async XLA Ops:
  6.5 4.7 %copy-start = (bf16[2048,4,128]{2,1,0:T(4,128)(2,1)S(1)}, bf16[2048,4,128]{2,1,0:T(4,128)(2,1)}, u32[]{:S(2)}) copy-start(bf16[2048,4,128]{2,1,0:T(4,128)(2,1)} %param.10) | copy-start | bytes 6291460
  6.5 85.7 %all-gather.2.cloned.1.call-start = ((), (), s32[]{:S(2)}) async-start(), calls=%async_computation | async-start | bytes 4718592 | tf_op jit(solution)/shard_map/all_gather | solution.py:11
  11.2 3.5 %copy-start.1 = (f32[4,2048,128,2]{2,1,3,0:T(8,128)}, f32[4,2048,128,2]{2,1,3,0:T(8,128)S(1)}, u32[]{:S(2)}) copy-start(f32[4,2048,128,2]{2,1,3,0:T(8,128)S(1)} %get-tuple-element.64) | copy-start | bytes 25165828
  15.9 127.2 %all-reduce.2.cloned.1.call-start = ((), (), s32[]{:S(2)}) async-start(), calls=%async_computation.1 | async-start | bytes 589824 | tf_op jit(solution)/shard_map/psum | solution.py:62
  93.3 72.2 %copy-start.2 = (f32[576]{0:T(1024)S(1)}, f32[576]{0:T(1024)}, u32[]{:S(2)}) copy-start(f32[576]{0:T(1024)} %param.13) | copy-start | bytes 6916
Sparse Core Ops, SparseCore 0:
  16.0 76.1 all-gather.1
  112.0 31.0 all-reduce.1
where the time goes:
time: 175 us; the launch traced here: 174 us
  blocking collectives  86.2 us (49%)
  waiting for transfers between devices  38.1 us (22%)
  other arithmetic  17.8 us (10%)
  between operations  14.3 us (8%)
  matrix products  9.75 us (6%)
  local copies, waits for them, and re-layouts  7.82 us (4%)
    all_gather x2, blocking collectives, merged(): pieces = jax.tree.map(lambda part: lax.all_gather(part, axis), value)  64.8 us
    psum x1, waiting for transfers between devices, body(): projected = lax.psum(projected_part, 'head')  31.2 us
    psum x1, blocking collectives, body(): square_total = lax.psum(square_part, 'seq')  21.4 us
    add x7, other arithmetic, combine_partials(): factor_former[..., None] * acc_former  10 us
    all_gather x1, waiting for transfers between devices, merged(): pieces = jax.tree.map(lambda part: lax.all_gather(part, axis), value)  6.87 us
    reduce_sum x1, other arithmetic, body(): block_sum = jnp.sum(weights, axis=-1)  4.59 us
    slice x3, local copies, waits for them, and re-layouts, merged(): tail = jax.tree.map(lambda part: part[1:], pieces)  4.08 us
    dot_general x1, matrix products, body(): jnp.einsum('tkgd,ckd->kgtc', grouped, key_cache, preferred_element_type=j...  3.86 us
  transfers between devices with their start and end apart: 2, of which 2 were waited for; matrix products, arithmetic and copies ran while one was open for 3% of the time, Pallas kernels for 0%

commit v1 on v0

--- a/solution.py
+++ b/solution.py
@@ -59,7 +59,11 @@
     projected_part = lax.dot_general(
         attention, out_weight, (((1,), (1,)), ((), ())), preferred_element_type=jnp.float32
     )
-    projected = lax.psum(projected_part, "head")
+    projected = projected_part
+    for hop in (1, 2):
+        projected = projected + lax.ppermute(
+            projected, "head", [(dev, dev ^ hop) for dev in range(4)]
+        )
     square_part = jnp.sum(projected * projected, axis=-1)
     square_total = lax.psum(square_part, "seq")
     mean_square = square_total / D

time: 175 us -> 149 us (0.85)
  waiting for transfers between devices: 38.1 us -> 16.1 us
  blocking collectives: 86.2 us -> 83.8 us
  other arithmetic: 17.8 us -> 15.9 us
    psum x1 -> x0, waiting for transfers between devices: 31.2 us -> none  [body(): projected = lax.psum(projected_part, 'head')]
    ppermute x0 -> x2, waiting for transfers between devices: none -> 9.15 us  [body(): lax.ppermute(projected, 'head', [(dev, dev ^ hop) for dev in range(4)])]
    psum x1, blocking collectives: 21.4 us -> 19 us  [body(): square_total = lax.psum(square_part, 'seq')]
  transfers between devices with their start and end apart: 2 -> 3, of which waited for: 2 -> 3; matrix products, arithmetic and copies ran while one was open for 3% -> 3% of each run, Pallas kernels for 0% -> 0%
where the time goes in v1:
time: 149 us
  blocking collectives  83.8 us (56%)
  waiting for transfers between devices  16.1 us (11%)
  other arithmetic  15.9 us (11%)
  between operations  14.3 us (10%)
  matrix products  9.05 us (6%)
  local copies, waits for them, and re-layouts  7.82 us (5%)
  starting transfers between devices  1.6 us (1%)
    all_gather x2, blocking collectives, merged(): pieces = jax.tree.map(lambda part: lax.all_gather(part, axis), value)  64.8 us
    psum x1, blocking collectives, body(): square_total = lax.psum(square_part, 'seq')  19 us
    add x7, other arithmetic, combine_partials(): factor_former[..., None] * acc_former  10 us
    ppermute x2, waiting for transfers between devices, body(): lax.ppermute(projected, 'head', [(dev, dev ^ hop) for dev in range(4)])  9.15 us
    all_gather x1, waiting for transfers between devices, merged(): pieces = jax.tree.map(lambda part: lax.all_gather(part, axis), value)  6.89 us
    reduce_sum x1, other arithmetic, body(): block_sum = jnp.sum(weights, axis=-1)  4.59 us
    slice x3, local copies, waits for them, and re-layouts, merged(): tail = jax.tree.map(lambda part: part[1:], pieces)  4.07 us
    dot_general x1, matrix products, body(): jnp.einsum('tkgd,ckd->kgtc', grouped, key_cache, preferred_element_type=j...  3.86 us
  transfers between devices with their start and end apart: 3, of which 3 were waited for; matrix products, arithmetic and copies ran while one was open for 3% of the time, Pallas kernels for 0%

profile of v1, /device:TPU:0, one launch (start us, length us, event | category | flops | bytes accessed | tf_op | source)
XLA Modules:
  0.0 148.7 jit_solution(13333628500634673263)
XLA Ops:
  7.4 3.9 %bitcast_reduce_fusion = (f32[4,2,128]{2,1,0:T(2,128)S(1)}, f32[4,2048,128,2]{2,1,3,0:T(8,128)S(1)}) fusion(pred[2048]{0:T(1024)(128)(4,1)S(1)} %iota_compare_fusion, bf16[128,4,2,128]{3,2,1,0:T(2,128)(2,1)} %bitcast.62, bf16[2048,4,128,1]{2,1,0,3:T(4,128)(2,1)} %bitcast.61), kind=kOutput, calls=%fused_computation.9 | convolution fusion | flops 543161344 | bytes 10754048 | tf_op jit(solution)/shard_map/tkgd,ckd->kgtc/dot_general | solution.py:36
  11.2 3.4 %fusion.7 = f32[4,2,128,128]{3,2,1,0:T(8,128)S(1)} fusion(f32[4,2048,128,2]{2,1,3,0:T(8,128)S(1)} %get-tuple-element.66, f32[4,2,128]{2,1,0:T(2,128)S(1)} %get-tuple-element.65, pred[2048]{0:T(1024)(128)(4,1)S(1)} %iota_compare_fusion, bf16[2048,4,128,1]{2,1,0,3:T(4,128)(2,1)S(1)} %bitcast.56), kind=kOutput, calls=%fused_computation.15 | convolution fusion | flops 547356672 | bytes 11016192 | tf_op jit(solution)/shard_map/kgtc,ckd->tkgd/dot_general | solution.py:45
  14.7 1.1 copy.21
  15.9 4.6 %fusion.6 = f32[4,2,128]{2,1,0:T(2,128)S(1)} fusion(f32[4,2048,128,2]{2,1,3,0:T(8,128)} %copy-done.1, f32[4,2,128]{2,1,0:T(2,128)S(1)} %get-tuple-element.65, pred[2048]{0:T(1024)(128)(4,1)S(1)} %iota_compare_fusion), kind=kLoop, calls=%fused_computation.14 | loop fusion | flops 10484736 | bytes 8398848 | tf_op jit(solution)/shard_map/reduce_sum | solution.py:43
  20.5 33.0 %all_gather.10 = f32[8,128,8]{1,2,0:T(8,128)S(1)} all-gather(f32[1,128,8]{1,2,0:T(8,128)S(1)} %bitcast.60), channel_id=1, replica_groups=mesh['seq'=8,'head'=4] {'seq'}, dimensions={0}, use_global_device_ids=true | all-gather | bytes 36864 | tf_op jit(solution)/shard_map/all_gather | solution.py:11
  53.5 31.8 %all_gather.9 = f32[8,128,8]{1,2,0:T(8,128)S(1)} all-gather(f32[1,128,8]{1,2,0:T(8,128)S(1)} %bitcast.59), channel_id=1, replica_groups=mesh['seq'=8,'head'=4] {'seq'}, dimensions={0}, use_global_device_ids=true | all-gather | bytes 36864 | tf_op jit(solution)/shard_map/all_gather | solution.py:11
  85.3 6.9 %all-gather.2.cloned.1.call-done = f32[8,128,8,128]{3,2,1,0:T(8,128)} async-done(((f32[1,128,8,128]{3,2,1,0:T(8,128)}), f32[8,128,8,128]{3,2,1,0:T(8,128)}) %all-gather.2.cloned.1.call-update) | async-done | bytes 4194320 | tf_op jit(solution)/shard_map/all_gather | solution.py:11
  92.2 1.1 slice_bitcast_fusion
  93.3 4.1 %slice.29 = f32[7,128,8,128]{3,2,1,0:T(8,128)} slice(f32[8,128,8,128]{3,2,1,0:T(8,128)} %all-gather.2.cloned.1.call-done), slice={[1:8], [0:128], [0:8], [0:128]} | slice | bytes 7340032 | tf_op jit(solution)/shard_map/slice | solution.py:13
  97.3 11.7 %while.14 = (s32[]{:T(128)}, f32[128,8]{0,1:T(8,128)S(1)}, f32[128,8]{0,1:T(8,128)S(1)}, f32[128,8,128]{2,1,0:T(8,128)S(1)}, f32[7,128,8]{1,2,0:T(8,128)S(1)}, /...) while((s32[]{:T(128)}, f32[128,8]{0,1:T(8,128)S(1)}, f32[128,8]{0,1:T(8,128)S(1)}, ...), condition=%wide.region_3.4_spmd, body=%wide.region_2.3_spmd.sunk | while | flops 399362 | bytes 1630309 | solution.py:14
  97.5 1.4 fusion.26
  99.2 1.4 fusion.26
  100.9 1.4 fusion.26
  102.6 1.4 fusion.26
  104.3 1.4 fusion.26
  105.9 1.4 fusion.26
  107.6 1.4 fusion.26
  109.2 0.2 divide_convert_fusion
  109.4 1.7 %fusion.14 = f32[128,576]{0,1:T(8,128)S(1)} fusion(bf16[576,1024]{1,0:T(8,128)(2,1)} %param.12, bf16[16,8,8,128]{3,2,1,0:T(8,128)(2,1)S(1)} %bitcast.57), kind=kOutput, calls=%fused_computation.25 | convolution fusion | flops 150994944 | bytes 1736704 | tf_op jit(solution)/shard_map/dot_general | solution.py:59
  111.2 1.6 %collective-permute-done = f32[128,576]{0,1:T(8,128)S(1)} collective-permute-done((f32[128,576]{0,1:T(8,128)S(1)}, f32[128,576]{0,1:T(8,128)S(1)}, u32[]{:S(2)}, u32[]{:S(2)}) %collective-permute-start) | collective-permute-done | bytes 294944 | tf_op jit(solution)/shard_map/ppermute | solution.py:64
  112.8 1.5 %collective-permute-start.1 = (f32[128,576]{0,1:T(8,128)S(1)}, f32[128,576]{0,1:T(8,128)S(1)}, u32[]{:S(2)}, u32[]{:S(2)}) collective-permute-start(f32[128,576]{0,1:T(8,128)S(1)} %add.23), channel_id=1, source_target_pairs={{0,2},{1,3},{2,0},{3,1},{4,6},{5,7},{6,4},{7,5},{8,10},{9,11},{10,... | collective-permute-start | bytes 884744 | tf_op jit(solution)/shard_map/ppermute | solution.py:64
  114.3 7.6 %collective-permute-done.1 = f32[128,576]{0,1:T(8,128)S(1)} collective-permute-done((f32[128,576]{0,1:T(8,128)S(1)}, f32[128,576]{0,1:T(8,128)S(1)}, u32[]{:S(2)}, u32[]{:S(2)}) %collective-permute-start.1) | collective-permute-done | bytes 294944 | tf_op jit(solution)/shard_map/ppermute | solution.py:64
  122.0 19.0 %psum.7 = f32[128]{0:T(128)S(1)} all-reduce(f32[128]{0:T(128)S(1)} %get-tuple-element.63), channel_id=1, replica_groups=mesh['seq'=8,'head'=4] {'seq'}, use_global_device_ids=true, to_apply=%region_5.6 | all-reduce | flops 128 | bytes 1024 | tf_op jit(solution)/shard_map/psum | solution.py:68
  141.1 0.8 multiply_convert_fusion
  (39 shorter events, 1.9 us)
Async XLA Ops:
  6.5 4.7 %copy-start = (bf16[2048,4,128]{2,1,0:T(4,128)(2,1)S(1)}, bf16[2048,4,128]{2,1,0:T(4,128)(2,1)}, u32[]{:S(2)}) copy-start(bf16[2048,4,128]{2,1,0:T(4,128)(2,1)} %param.10) | copy-start | bytes 6291460
  6.5 85.6 %all-gather.2.cloned.1.call-start = ((), (), s32[]{:S(2)}) async-start(), calls=%async_computation | async-start | bytes 4718592 | tf_op jit(solution)/shard_map/all_gather | solution.py:11
  11.2 3.5 %copy-start.1 = (f32[4,2048,128,2]{2,1,3,0:T(8,128)}, f32[4,2048,128,2]{2,1,3,0:T(8,128)S(1)}, u32[]{:S(2)}) copy-start(f32[4,2048,128,2]{2,1,3,0:T(8,128)S(1)} %get-tuple-element.66) | copy-start | bytes 25165828
  97.3 43.7 %copy-start.2 = (f32[576]{0:T(1024)S(1)}, f32[576]{0:T(1024)}, u32[]{:S(2)}) copy-start(f32[576]{0:T(1024)} %param.13) | copy-start | bytes 6916
  111.1 1.6 %collective-permute-start = (f32[128,576]{0,1:T(8,128)S(1)}, f32[128,576]{0,1:T(8,128)S(1)}, u32[]{:S(2)}, u32[]{:S(2)}) collective-permute-start(f32[128,576]{0,1:T(8,128)S(1)} %fusion.14), channel_id=1, source_target_pairs={{0,1},{1,0},{2,3},{3,2},{4,5},{5,4},{6,7},{7,6},{8,9},{9,8},{10,11... | collective-permute-start | bytes 884744 | tf_op jit(solution)/shard_map/ppermute | solution.py:64
  112.8 9.1 %collective-permute-start.1 = (f32[128,576]{0,1:T(8,128)S(1)}, f32[128,576]{0,1:T(8,128)S(1)}, u32[]{:S(2)}, u32[]{:S(2)}) collective-permute-start(f32[128,576]{0,1:T(8,128)S(1)} %add.23), channel_id=1, source_target_pairs={{0,2},{1,3},{2,0},{3,1},{4,6},{5,7},{6,4},{7,5},{8,10},{9,11},{10,... | collective-permute-start | bytes 884744 | tf_op jit(solution)/shard_map/ppermute | solution.py:64
Sparse Core Ops, SparseCore 0:
  16.0 76.1 all-gather.1
